TPU v7x, 32 devices: a whole 2x2x4 slice. The times are simulated.
32 devices in a mesh: gx: 2 (over x), gy: 16 (over z, y, core).
Axes of the slice: x: 2, y: 2, z: 4, core: 2. Of those that a mesh axis runs over, the one named last changes fastest.
Arguments:
- right_side: float32 [262144], P(('gx', 'gy')), may hold values from -60 to 60
- reaction: float32 [262144], P(('gx', 'gy')), may hold values from 0.5 to 2
- cell_slots: int32 [125, 4096], P(None, ('gx', 'gy')), may hold values from 0 to 12543
- cell_level: int32 [4096], P(('gx', 'gy')), may hold values from 0 to 2
- con_masters: int32 [5, 8192], P(None, ('gx', 'gy')), may hold values from 0 to 12287
- con_rows: int32 [8192], P(('gx', 'gy')), may hold values from 0 to 9
- send_lists: int32 [8, 16384], P(None, ('gx', 'gy')), may hold values from 0 to 8191
Outputs:
- solution: float32 [262144], P(('gx', 'gy'))
- residual: float32 [262144], P(('gx', 'gy'))
Inputs may be any that keep to these rules, and one draw needn't show every extreme that they name: `cell_slots`: column block of rank d indexes d's local list: its 8192 owned unknowns, then 512 values from each of ranks d - 1, ..., d - 4, then from d + 1, ..., d + 4, then its 256 constrained values (rank d = 16 gx + gy). `cell_level`: A cell of level l has side 2^(-l). `con_masters`: slots among the same rank's owned and ghost values. `con_rows`: row of the interpolation table: 5 fine nodes on each half of a coarse edge. `send_lists`: row j of rank s lists s's owned unknowns that fill ghost block j of rank s + j + 1 (j < 4) or of rank s - (j - 3); rows without such a rank are unused.
All inputs are finite; a program needn't handle non-finite values.
Results may differ from a plain program's by a relative error of at most 0.0002.
Values sent between devices are 32-bit elements; how exact they have to be, the bound alone decides.
A program may use at most 64 MiB of HBM per device.

v0:
```python
import jax
import jax.numpy as jnp
import numpy as np
from jax import lax
from jax.sharding import PartitionSpec as P

ITERS = 3


def shifted(value, axis, steps):
    count = lax.axis_size(axis)
    initial, last = (max(0, -steps), min(count, count - steps))
    return lax.ppermute(value, axis, [(source, source + steps) for source in range(initial, last)])


def lagrange(node_list, points):
    node_count = len(node_list)
    values = np.ones((len(points), node_count))
    derivs = np.zeros((len(points), node_count))
    for basis_node in range(node_count):
        for other_node in range(node_count):
            if other_node != basis_node:
                values[:, basis_node] = (
                    values[:, basis_node]
                    * (points - node_list[other_node])
                    / (node_list[basis_node] - node_list[other_node])
                )
        for skipped in range(node_count):
            if skipped != basis_node:
                product_term = np.ones(len(points)) / (node_list[basis_node] - node_list[skipped])
                for other_node in range(node_count):
                    if other_node != basis_node and other_node != skipped:
                        product_term = (
                            product_term
                            * (points - node_list[other_node])
                            / (node_list[basis_node] - node_list[other_node])
                        )
                derivs[:, basis_node] = derivs[:, basis_node] + product_term
    return (values, derivs)


def tables():
    gll_offset = np.sqrt(3.0 / 7.0)
    lobatto = np.array([0.0, (1.0 - gll_offset) / 2.0, 0.5, (1.0 + gll_offset) / 2.0, 1.0])
    inner_point = np.sqrt(5.0 - 2.0 * np.sqrt(10.0 / 7.0)) / 3.0
    outer_point = np.sqrt(5.0 + 2.0 * np.sqrt(10.0 / 7.0)) / 3.0
    inner_weight = (322.0 + 13.0 * np.sqrt(70.0)) / 900.0
    outer_weight = (322.0 - 13.0 * np.sqrt(70.0)) / 900.0
    points = np.array([-outer_point, -inner_point, 0.0, inner_point, outer_point])
    gauss_weights = np.array(
        [outer_weight, inner_weight, 128.0 / 225.0, inner_weight, outer_weight]
    )
    points = (points + 1.0) / 2.0
    gauss_weights = gauss_weights / 2.0
    shapes, slopes = lagrange(lobatto, points)
    fine_points = np.concatenate([lobatto / 2.0, (1.0 + lobatto) / 2.0])
    interp, unused_slopes = lagrange(lobatto, fine_points)
    quad_weights = np.kron(gauss_weights, np.kron(gauss_weights, gauss_weights))
    grad_x = np.kron(slopes, np.kron(shapes, shapes))
    grad_y = np.kron(shapes, np.kron(slopes, shapes))
    grad_z = np.kron(shapes, np.kron(shapes, slopes))
    stiffness = np.zeros((125, 125))
    for gradient in (grad_x, grad_y, grad_z):
        stiffness = stiffness + gradient.T @ (quad_weights[:, None] * gradient)
    return (jnp.asarray(interp, jnp.float32), jnp.asarray(stiffness, jnp.float32))


def cell_laplace(cell_values, cell_scale, stiffness):
    product = jnp.dot(
        stiffness, cell_values, precision=lax.Precision.HIGHEST, preferred_element_type=jnp.float32
    )
    return product * cell_scale[None, :]


def local_apply(own_values, ghosts, slot_map, cell_scale, masters, weights, stiffness):
    local_list = jnp.concatenate([own_values, ghosts.reshape(-1)])
    picked = local_list[masters]
    resolved = jnp.sum(weights * picked, axis=0)
    full_list = jnp.concatenate([local_list, resolved])
    cell_values = full_list[slot_map]
    contrib = cell_laplace(cell_values, cell_scale, stiffness)
    summed = (
        jnp.zeros(full_list.shape, jnp.float32).at[slot_map.reshape(-1)].add(contrib.reshape(-1))
    )
    split_at = local_list.shape[0]
    spread = (
        summed[:split_at]
        .at[masters.reshape(-1)]
        .add((weights * summed[split_at:][None, :]).reshape(-1))
    )
    return spread


def on_device(right_side, reaction, cell_slots, cell_level, con_masters, con_rows, send_lists):
    interp, stiffness = tables()
    block_count = send_lists.shape[0]
    half_count = block_count // 2
    offsets = [neighbour + 1 for neighbour in range(half_count)] + [
        -(neighbour + 1) for neighbour in range(half_count)
    ]
    cell_scale = jnp.exp2(-cell_level.astype(jnp.float32))
    selector = (con_rows[None, :] == jnp.arange(10, dtype=jnp.int32)[:, None]).astype(jnp.float32)
    weights = jnp.dot(interp.T, selector, precision=lax.Precision.HIGHEST)
    own_count = right_side.shape[0]
    flat_lists = send_lists.reshape(-1)

    def carry_out(packed):
        return jnp.stack(
            [
                shifted(packed[neighbour], ("gx", "gy"), offsets[neighbour])
                for neighbour in range(block_count)
            ]
        )

    def carry_back(packed):
        return jnp.stack(
            [
                shifted(packed[neighbour], ("gx", "gy"), -offsets[neighbour])
                for neighbour in range(block_count)
            ]
        )

    def operate(vector):
        ghosts = carry_out(vector[send_lists])
        spread = local_apply(
            vector, ghosts, cell_slots, cell_scale, con_masters, weights, stiffness
        )
        returned = carry_back(spread[own_count:].reshape(block_count, -1))
        result = spread[:own_count] + reaction * vector
        return result.at[flat_lists].add(returned.reshape(-1))

    def paired_sums(vector, applied):
        return lax.psum((jnp.sum(vector * vector), jnp.sum(vector * applied)), ("gx", "gy"))

    solution = jnp.zeros_like(right_side)
    residual = right_side
    applied = operate(residual)
    norm_now, product = paired_sums(residual, applied)
    step_size = norm_now / product
    direction = residual
    applied_dir = applied
    for iteration in range(ITERS):
        solution = solution + step_size * direction
        residual = residual - step_size * applied_dir
        if iteration + 1 < ITERS:
            applied = operate(residual)
            norm_next, product = paired_sums(residual, applied)
            beta_ratio = norm_next / norm_now
            step_size = norm_next / (product - beta_ratio * norm_next / step_size)
            direction = residual + beta_ratio * direction
            applied_dir = applied + beta_ratio * applied_dir
            norm_now = norm_next
    return (solution, residual)


def solution(mesh):
    placed = (
        P(("gx", "gy")),
        P(("gx", "gy")),
        P(None, ("gx", "gy")),
        P(("gx", "gy")),
        P(None, ("gx", "gy")),
        P(("gx", "gy")),
        P(None, ("gx", "gy")),
    )
    return jax.shard_map(
        on_device,
        mesh=mesh,
        in_specs=placed,
        out_specs=(P(("gx", "gy")), P(("gx", "gy"))),
        check_vma=False,
    )
```

profile of v0, /device:TPU:0, one launch (start us, length us, event | category | flops | bytes accessed | tf_op | source)
XLA Modules:
  0.0 995.8 jit_solution(12732455110175397359)
XLA Ops:
  2.1 23.0 %gather_fusion = f32[4096]{0:T(1024)S(1)} fusion(f32[8192]{0:T(1024)S(1)} %copy-done, s32[4096]{0:T(1024)S(1)} %broadcast_clamp_fusion), kind=kCustom, calls=%fused_computation | custom fusion | bytes 49152 | tf_op jit(solution)/shard_map/gather | solution.py:124
  30.4 7.7 collective-permute-start.3
  49.8 7.1 gather_fusion.1
  57.9 82.3 %gather_fusion.2 = f32[16000]{0:T(1024)S(1)} fusion(f32[12544]{0:T(1024)S(1)} %pad_maximum_fusion, s32[16384]{0:T(1024)S(1)} %pad_clamp_fusion), kind=kCustom, calls=%fused_computation.2 | custom fusion | bytes 192000 | tf_op jit(solution)/shard_map/gather | solution.py:80
  140.6 85.1 %scatter_custom_fusion = f32[12544]{0:T(1024)S(1)} fusion(s32[16000]{0:T(1024)S(1)} %fusion.7, f32[16000]{0:T(1024)S(1)} %bitcast.115, f32[]{:T(128)} %constant.8.clone.1), kind=kCustom, calls=%fused_computation.59 | custom fusion | flops 16000 | bytes 50180 | tf_op jit(solution)/shard_map/scatter-add | solution.py:83
  225.8 7.4 scatter_fusion
  258.6 22.5 %scatter_fusion.1 = f32[8192]{0:T(1024)S(1)} fusion(f32[8192]{0:T(1024)S(1)} %slice_add_fusion.2, s32[4096]{0:T(1024)S(1)} %bitcast.101, f32[4096]{0:T(1024)S(1)} %bitcast.112), kind=kCustom, calls=%fused_computation.11 | custom fusion | flops 4096 | bytes 65536 | tf_op jit(solution)/shard_map/scatter-add | solution.py:130
  281.7 50.0 %all-reduce.2 = (f32[]{:T(128)}, f32[]{:T(128)}) all-reduce(f32[]{:T(128)} %get-tuple-element.7, f32[]{:T(128)} %get-tuple-element.6), channel_id=1, replica_groups=mesh['gx'=2,'gy'=16] {'gx','gy'}, use_global_device_ids=true, to_apply=%region_1.0 | all-reduce | flops 2 | bytes 16 | tf_op jit(solution)/shard_map/psum | solution.py:133
  333.0 23.0 %gather_fusion.3 = f32[4096]{0:T(1024)S(1)} fusion(f32[8192]{0:T(1024)S(1)} %multiply_subtract_fusion.2, s32[4096]{0:T(1024)S(1)} %broadcast_clamp_fusion), kind=kCustom, calls=%fused_computation.3 | custom fusion | bytes 49152 | tf_op jit(solution)/shard_map/gather | solution.py:124
  361.3 7.1 collective-permute-start.19
  380.0 7.1 gather_fusion.4
  387.1 82.3 %gather_fusion.5 = f32[16000]{0:T(1024)S(1)} fusion(f32[12544]{0:T(1024)S(1)} %pad_maximum_fusion.1, s32[16384]{0:T(1024)S(1)} %pad_clamp_fusion), kind=kCustom, calls=%fused_computation.5 | custom fusion | bytes 192000 | tf_op jit(solution)/shard_map/gather | solution.py:80
  469.8 85.1 %scatter_custom_fusion.3 = f32[12544]{0:T(1024)S(1)} fusion(s32[16000]{0:T(1024)S(1)} %fusion.7, f32[16000]{0:T(1024)S(1)} %bitcast.116, f32[]{:T(128)} %constant.8.clone.1), kind=kCustom, calls=%fused_computation.57 | custom fusion | flops 16000 | bytes 50180 | tf_op jit(solution)/shard_map/scatter-add | solution.py:83
  555.0 7.6 scatter_fusion.2
  588.0 22.5 %scatter_fusion.3 = f32[8192]{0:T(1024)S(1)} fusion(f32[8192]{0:T(1024)S(1)} %slice_add_fusion.1, s32[4096]{0:T(1024)S(1)} %bitcast.102, f32[4096]{0:T(1024)S(1)} %bitcast.113), kind=kCustom, calls=%fused_computation.14 | custom fusion | flops 4096 | bytes 65536 | tf_op jit(solution)/shard_map/scatter-add | solution.py:130
  611.1 48.9 %all-reduce.1 = (f32[]{:T(128)}, f32[]{:T(128)}) all-reduce(f32[]{:T(128)} %get-tuple-element.5, f32[]{:T(128)} %get-tuple-element.4), channel_id=1, replica_groups=mesh['gx'=2,'gy'=16] {'gx','gy'}, use_global_device_ids=true, to_apply=%region_9.0 | all-reduce | flops 2 | bytes 16 | tf_op jit(solution)/shard_map/psum | solution.py:133
  664.5 23.0 %gather_fusion.6 = f32[4096]{0:T(1024)S(1)} fusion(f32[8192]{0:T(1024)S(1)} %multiply_subtract_fusion.1, s32[4096]{0:T(1024)S(1)} %broadcast_clamp_fusion), kind=kCustom, calls=%fused_computation.6 | custom fusion | bytes 49152 | tf_op jit(solution)/shard_map/gather | solution.py:124
  692.7 7.1 collective-permute-start.35
  711.4 7.1 gather_fusion.7
  718.6 82.3 %gather_fusion.8 = f32[16000]{0:T(1024)S(1)} fusion(f32[12544]{0:T(1024)S(1)} %pad_maximum_fusion.2, s32[16384]{0:T(1024)S(1)} %pad_clamp_fusion), kind=kCustom, calls=%fused_computation.8 | custom fusion | bytes 192000 | tf_op jit(solution)/shard_map/gather | solution.py:80
  801.3 85.1 %scatter_custom_fusion.6 = f32[12544]{0:T(1024)S(1)} fusion(s32[16000]{0:T(1024)S(1)} %fusion.7, f32[16000]{0:T(1024)S(1)} %bitcast.114, f32[]{:T(128)} %constant.8.clone.1), kind=kCustom, calls=%fused_computation.55 | custom fusion | flops 16000 | bytes 50180 | tf_op jit(solution)/shard_map/scatter-add | solution.py:83
  886.5 7.4 scatter_fusion.4
  919.3 22.5 %scatter_fusion.5 = f32[8192]{0:T(1024)S(1)} fusion(f32[8192]{0:T(1024)S(1)} %slice_add_fusion, s32[4096]{0:T(1024)S(1)} %bitcast.103, f32[4096]{0:T(1024)S(1)} %bitcast.111), kind=kCustom, calls=%fused_computation.17 | custom fusion | flops 4096 | bytes 65536 | tf_op jit(solution)/shard_map/scatter-add | solution.py:130
  942.4 48.9 %all-reduce = (f32[]{:T(128)}, f32[]{:T(128)}) all-reduce(f32[]{:T(128)} %get-tuple-element.3, f32[]{:T(128)} %get-tuple-element.2), channel_id=1, replica_groups=mesh['gx'=2,'gy'=16] {'gx','gy'}, use_global_device_ids=true, to_apply=%region_17.0 | all-reduce | flops 2 | bytes 16 | tf_op jit(solution)/shard_map/psum | solution.py:133
  (182 shorter events, 132.1 us)
Async XLA Ops:
  25.2 13.3 %collective-permute-start.7 = (f32[512]{0:T(512)S(1)}, f32[512]{0:T(512)S(1)}, u32[]{:S(2)}, u32[]{:S(2)}) collective-permute-start(f32[512]{0:T(512)S(1)} %get-tuple-element.56), channel_id=1, source_target_pairs={{4,0},{5,1},{6,2},{7,3},{8,4},{9,5},{10,6},{11,7},{12,8},{13,9},{1... | collective-permute-start | bytes 6152 | tf_op jit(solution)/shard_map/ppermute | solution.py:13
  26.5 15.6 %collective-permute-start.6 = (f32[512]{0:T(512)S(1)}, f32[512]{0:T(512)S(1)}, u32[]{:S(2)}, u32[]{:S(2)}) collective-permute-start(f32[512]{0:T(512)S(1)} %get-tuple-element.57), channel_id=1, source_target_pairs={{3,0},{4,1},{5,2},{6,3},{7,4},{8,5},{9,6},{10,7},{11,8},{12,9},{13... | collective-permute-start | bytes 6152 | tf_op jit(solution)/shard_map/ppermute | solution.py:13
  27.8 19.0 %collective-permute-start.5 = (f32[512]{0:T(512)S(1)}, f32[512]{0:T(512)S(1)}, u32[]{:S(2)}, u32[]{:S(2)}) collective-permute-start(f32[512]{0:T(512)S(1)} %get-tuple-element.58), channel_id=1, source_target_pairs={{2,0},{3,1},{4,2},{5,3},{6,4},{7,5},{8,6},{9,7},{10,8},{11,9},{12,... | collective-permute-start | bytes 6152 | tf_op jit(solution)/shard_map/ppermute | solution.py:13
  29.1 20.0 %collective-permute-start.4 = (f32[512]{0:T(512)S(1)}, f32[512]{0:T(512)S(1)}, u32[]{:S(2)}, u32[]{:S(2)}) collective-permute-start(f32[512]{0:T(512)S(1)} %get-tuple-element.59), channel_id=1, source_target_pairs={{1,0},{2,1},{3,2},{4,3},{5,4},{6,5},{7,6},{8,7},{9,8},{10,9},{11,1... | collective-permute-start | bytes 6152 | tf_op jit(solution)/shard_map/ppermute | solution.py:13
  30.4 18.7 %collective-permute-start.3 = (f32[512]{0:T(512)S(1)}, f32[512]{0:T(512)S(1)}, u32[]{:S(2)}, u32[]{:S(2)}) collective-permute-start(f32[512]{0:T(512)S(1)} %get-tuple-element.60), channel_id=1, source_target_pairs={{0,4},{1,5},{2,6},{3,7},{4,8},{5,9},{6,10},{7,11},{8,12},{9,13},{1... | collective-permute-start | bytes 6152 | tf_op jit(solution)/shard_map/ppermute | solution.py:13
  38.4 10.6 %collective-permute-start.2 = (f32[512]{0:T(512)S(1)}, f32[512]{0:T(512)S(1)}, u32[]{:S(2)}, u32[]{:S(2)}) collective-permute-start(f32[512]{0:T(512)S(1)} %get-tuple-element.61), channel_id=1, source_target_pairs={{0,3},{1,4},{2,5},{3,6},{4,7},{5,8},{6,9},{7,10},{8,11},{9,12},{10... | collective-permute-start | bytes 6152 | tf_op jit(solution)/shard_map/ppermute | solution.py:13
  233.3 18.1 %collective-permute-start.15 = (f32[512]{0:T(512)S(1)}, f32[512]{0:T(512)S(1)}, u32[]{:S(2)}, u32[]{:S(2)}) collective-permute-start(f32[512]{0:T(512)S(1)} %get-tuple-element.30), channel_id=1, source_target_pairs={{0,4},{1,5},{2,6},{3,7},{4,8},{5,9},{6,10},{7,11},{8,12},{9,13},{1... | collective-permute-start | bytes 6152 | tf_op jit(solution)/shard_map/ppermute | solution.py:13
  239.6 13.1 %collective-permute-start.14 = (f32[512]{0:T(512)S(1)}, f32[512]{0:T(512)S(1)}, u32[]{:S(2)}, u32[]{:S(2)}) collective-permute-start(f32[512]{0:T(512)S(1)} %get-tuple-element.31), channel_id=1, source_target_pairs={{0,3},{1,4},{2,5},{3,6},{4,7},{5,8},{6,9},{7,10},{8,11},{9,12},{10... | collective-permute-start | bytes 6152 | tf_op jit(solution)/shard_map/ppermute | solution.py:13
  356.1 12.3 %collective-permute-start.23 = (f32[512]{0:T(512)S(1)}, f32[512]{0:T(512)S(1)}, u32[]{:S(2)}, u32[]{:S(2)}) collective-permute-start(f32[512]{0:T(512)S(1)} %get-tuple-element.48), channel_id=1, source_target_pairs={{4,0},{5,1},{6,2},{7,3},{8,4},{9,5},{10,6},{11,7},{12,8},{13,9},{1... | collective-permute-start | bytes 6152 | tf_op jit(solution)/shard_map/ppermute | solution.py:13
  357.4 14.7 %collective-permute-start.22 = (f32[512]{0:T(512)S(1)}, f32[512]{0:T(512)S(1)}, u32[]{:S(2)}, u32[]{:S(2)}) collective-permute-start(f32[512]{0:T(512)S(1)} %get-tuple-element.49), channel_id=1, source_target_pairs={{3,0},{4,1},{5,2},{6,3},{7,4},{8,5},{9,6},{10,7},{11,8},{12,9},{13... | collective-permute-start | bytes 6152 | tf_op jit(solution)/shard_map/ppermute | solution.py:13
  358.7 18.2 %collective-permute-start.21 = (f32[512]{0:T(512)S(1)}, f32[512]{0:T(512)S(1)}, u32[]{:S(2)}, u32[]{:S(2)}) collective-permute-start(f32[512]{0:T(512)S(1)} %get-tuple-element.50), channel_id=1, source_target_pairs={{2,0},{3,1},{4,2},{5,3},{6,4},{7,5},{8,6},{9,7},{10,8},{11,9},{12,... | collective-permute-start | bytes 6152 | tf_op jit(solution)/shard_map/ppermute | solution.py:13
  360.0 19.1 %collective-permute-start.20 = (f32[512]{0:T(512)S(1)}, f32[512]{0:T(512)S(1)}, u32[]{:S(2)}, u32[]{:S(2)}) collective-permute-start(f32[512]{0:T(512)S(1)} %get-tuple-element.51), channel_id=1, source_target_pairs={{1,0},{2,1},{3,2},{4,3},{5,4},{6,5},{7,6},{8,7},{9,8},{10,9},{11,1... | collective-permute-start | bytes 6152 | tf_op jit(solution)/shard_map/ppermute | solution.py:13
  361.3 17.8 %collective-permute-start.19 = (f32[512]{0:T(512)S(1)}, f32[512]{0:T(512)S(1)}, u32[]{:S(2)}, u32[]{:S(2)}) collective-permute-start(f32[512]{0:T(512)S(1)} %get-tuple-element.52), channel_id=1, source_target_pairs={{0,4},{1,5},{2,6},{3,7},{4,8},{5,9},{6,10},{7,11},{8,12},{9,13},{1... | collective-permute-start | bytes 6152 | tf_op jit(solution)/shard_map/ppermute | solution.py:13
  368.4 10.7 %collective-permute-start.18 = (f32[512]{0:T(512)S(1)}, f32[512]{0:T(512)S(1)}, u32[]{:S(2)}, u32[]{:S(2)}) collective-permute-start(f32[512]{0:T(512)S(1)} %get-tuple-element.53), channel_id=1, source_target_pairs={{0,3},{1,4},{2,5},{3,6},{4,7},{5,8},{6,9},{7,10},{8,11},{9,12},{10... | collective-permute-start | bytes 6152 | tf_op jit(solution)/shard_map/ppermute | solution.py:13
  562.6 18.5 %collective-permute-start.31 = (f32[512]{0:T(512)S(1)}, f32[512]{0:T(512)S(1)}, u32[]{:S(2)}, u32[]{:S(2)}) collective-permute-start(f32[512]{0:T(512)S(1)} %get-tuple-element.22), channel_id=1, source_target_pairs={{0,4},{1,5},{2,6},{3,7},{4,8},{5,9},{6,10},{7,11},{8,12},{9,13},{1... | collective-permute-start | bytes 6152 | tf_op jit(solution)/shard_map/ppermute | solution.py:13
  569.4 13.1 %collective-permute-start.30 = (f32[512]{0:T(512)S(1)}, f32[512]{0:T(512)S(1)}, u32[]{:S(2)}, u32[]{:S(2)}) collective-permute-start(f32[512]{0:T(512)S(1)} %get-tuple-element.23), channel_id=1, source_target_pairs={{0,3},{1,4},{2,5},{3,6},{4,7},{5,8},{6,9},{7,10},{8,11},{9,12},{10... | collective-permute-start | bytes 6152 | tf_op jit(solution)/shard_map/ppermute | solution.py:13
  687.5 12.3 %collective-permute-start.39 = (f32[512]{0:T(512)S(1)}, f32[512]{0:T(512)S(1)}, u32[]{:S(2)}, u32[]{:S(2)}) collective-permute-start(f32[512]{0:T(512)S(1)} %get-tuple-element.40), channel_id=1, source_target_pairs={{4,0},{5,1},{6,2},{7,3},{8,4},{9,5},{10,6},{11,7},{12,8},{13,9},{1... | collective-permute-start | bytes 6152 | tf_op jit(solution)/shard_map/ppermute | solution.py:13
  688.8 14.7 %collective-permute-start.38 = (f32[512]{0:T(512)S(1)}, f32[512]{0:T(512)S(1)}, u32[]{:S(2)}, u32[]{:S(2)}) collective-permute-start(f32[512]{0:T(512)S(1)} %get-tuple-element.41), channel_id=1, source_target_pairs={{3,0},{4,1},{5,2},{6,3},{7,4},{8,5},{9,6},{10,7},{11,8},{12,9},{13... | collective-permute-start | bytes 6152 | tf_op jit(solution)/shard_map/ppermute | solution.py:13
  690.1 18.2 %collective-permute-start.37 = (f32[512]{0:T(512)S(1)}, f32[512]{0:T(512)S(1)}, u32[]{:S(2)}, u32[]{:S(2)}) collective-permute-start(f32[512]{0:T(512)S(1)} %get-tuple-element.42), channel_id=1, source_target_pairs={{2,0},{3,1},{4,2},{5,3},{6,4},{7,5},{8,6},{9,7},{10,8},{11,9},{12,... | collective-permute-start | bytes 6152 | tf_op jit(solution)/shard_map/ppermute | solution.py:13
  691.4 19.1 %collective-permute-start.36 = (f32[512]{0:T(512)S(1)}, f32[512]{0:T(512)S(1)}, u32[]{:S(2)}, u32[]{:S(2)}) collective-permute-start(f32[512]{0:T(512)S(1)} %get-tuple-element.43), channel_id=1, source_target_pairs={{1,0},{2,1},{3,2},{4,3},{5,4},{6,5},{7,6},{8,7},{9,8},{10,9},{11,1... | collective-permute-start | bytes 6152 | tf_op jit(solution)/shard_map/ppermute | solution.py:13
  692.7 17.8 %collective-permute-start.35 = (f32[512]{0:T(512)S(1)}, f32[512]{0:T(512)S(1)}, u32[]{:S(2)}, u32[]{:S(2)}) collective-permute-start(f32[512]{0:T(512)S(1)} %get-tuple-element.44), channel_id=1, source_target_pairs={{0,4},{1,5},{2,6},{3,7},{4,8},{5,9},{6,10},{7,11},{8,12},{9,13},{1... | collective-permute-start | bytes 6152 | tf_op jit(solution)/shard_map/ppermute | solution.py:13
  699.8 10.7 %collective-permute-start.34 = (f32[512]{0:T(512)S(1)}, f32[512]{0:T(512)S(1)}, u32[]{:S(2)}, u32[]{:S(2)}) collective-permute-start(f32[512]{0:T(512)S(1)} %get-tuple-element.45), channel_id=1, source_target_pairs={{0,3},{1,4},{2,5},{3,6},{4,7},{5,8},{6,9},{7,10},{8,11},{9,12},{10... | collective-permute-start | bytes 6152 | tf_op jit(solution)/shard_map/ppermute | solution.py:13
  893.9 18.5 %collective-permute-start.47 = (f32[512]{0:T(512)S(1)}, f32[512]{0:T(512)S(1)}, u32[]{:S(2)}, u32[]{:S(2)}) collective-permute-start(f32[512]{0:T(512)S(1)} %get-tuple-element.14), channel_id=1, source_target_pairs={{0,4},{1,5},{2,6},{3,7},{4,8},{5,9},{6,10},{7,11},{8,12},{9,13},{1... | collective-permute-start | bytes 6152 | tf_op jit(solution)/shard_map/ppermute | solution.py:13
  900.7 13.1 %collective-permute-start.46 = (f32[512]{0:T(512)S(1)}, f32[512]{0:T(512)S(1)}, u32[]{:S(2)}, u32[]{:S(2)}) collective-permute-start(f32[512]{0:T(512)S(1)} %get-tuple-element.15), channel_id=1, source_target_pairs={{0,3},{1,4},{2,5},{3,6},{4,7},{5,8},{6,9},{7,10},{8,11},{9,12},{10... | collective-permute-start | bytes 6152 | tf_op jit(solution)/shard_map/ppermute | solution.py:13
  (33 other events, 349.3 us)
where the time goes:
time: 998 us; the launch traced here: 996 us
  other arithmetic  349 us (35%)
  local copies, waits for them, and re-layouts  339 us (34%)
  blocking collectives  148 us (15%)
  starting transfers between devices  136 us (14%)
  between operations  11.6 us (1%)
  waiting for transfers between devices  11.3 us (1%)
    scatter-add x3, other arithmetic, local_apply(): jnp.zeros(full_list.shape, jnp.float32).at[slot_map.reshape(-1)]  255 us
    gather x3, local copies, waits for them, and re-layouts, local_apply(): cell_values = full_list[slot_map]  247 us
    psum x3, blocking collectives, paired_sums(): lax.psum((jnp.sum(vector * vector), jnp.sum(vector * applied)), ('gx', 'g...  148 us
    ppermute x48, starting transfers between devices, shifted(): lax.ppermute(value, axis, [(source, source + steps) for source in range(i...  136 us
    gather x3, local copies, waits for them, and re-layouts, operate(): ghosts = carry_out(vector[send_lists])  69.1 us
    scatter-add x3, other arithmetic, operate(): return result.at[flat_lists].add(returned.reshape(-1))  67.4 us
    scatter-add x3, other arithmetic, local_apply(): spread = summed[:split_at].at[masters.reshape(-1)].add((weights * summed[...  22.4 us
    gather x6, local copies, waits for them, and re-layouts, local_apply(): picked = local_list[masters]  21.3 us
  transfers between devices with their start and end apart: 48, of which 12 were waited for; matrix products, arithmetic and copies ran while one was open for 0% of the time, Pallas kernels for 0%

commit v1 on v0

v1 whole, which is shorter than its diff:
```python
import functools

import jax
import jax.numpy as jnp
import numpy as np
from jax import lax
from jax.experimental import pallas as pl
from jax.experimental.pallas import tpu as pltpu
from jax.sharding import PartitionSpec as P

ITERS = 3
LANES = 128
MESH = pl.DeviceIdType.MESH


def lagrange(node_list, points):
    node_count = len(node_list)
    values = np.ones((len(points), node_count))
    derivs = np.zeros((len(points), node_count))
    for basis_node in range(node_count):
        for other_node in range(node_count):
            if other_node != basis_node:
                values[:, basis_node] = (
                    values[:, basis_node]
                    * (points - node_list[other_node])
                    / (node_list[basis_node] - node_list[other_node])
                )
        for skipped in range(node_count):
            if skipped != basis_node:
                product_term = np.ones(len(points)) / (node_list[basis_node] - node_list[skipped])
                for other_node in range(node_count):
                    if other_node != basis_node and other_node != skipped:
                        product_term = (
                            product_term
                            * (points - node_list[other_node])
                            / (node_list[basis_node] - node_list[other_node])
                        )
                derivs[:, basis_node] = derivs[:, basis_node] + product_term
    return (values, derivs)


def tables():
    gll_offset = np.sqrt(3.0 / 7.0)
    lobatto = np.array([0.0, (1.0 - gll_offset) / 2.0, 0.5, (1.0 + gll_offset) / 2.0, 1.0])
    inner_point = np.sqrt(5.0 - 2.0 * np.sqrt(10.0 / 7.0)) / 3.0
    outer_point = np.sqrt(5.0 + 2.0 * np.sqrt(10.0 / 7.0)) / 3.0
    inner_weight = (322.0 + 13.0 * np.sqrt(70.0)) / 900.0
    outer_weight = (322.0 - 13.0 * np.sqrt(70.0)) / 900.0
    points = np.array([-outer_point, -inner_point, 0.0, inner_point, outer_point])
    gauss_weights = np.array(
        [outer_weight, inner_weight, 128.0 / 225.0, inner_weight, outer_weight]
    )
    points = (points + 1.0) / 2.0
    gauss_weights = gauss_weights / 2.0
    shapes, slopes = lagrange(lobatto, points)
    fine_points = np.concatenate([lobatto / 2.0, (1.0 + lobatto) / 2.0])
    interp, unused_slopes = lagrange(lobatto, fine_points)
    quad_weights = np.kron(gauss_weights, np.kron(gauss_weights, gauss_weights))
    grad_x = np.kron(slopes, np.kron(shapes, shapes))
    grad_y = np.kron(shapes, np.kron(slopes, shapes))
    grad_z = np.kron(shapes, np.kron(shapes, slopes))
    stiffness = np.zeros((125, 125))
    for gradient in (grad_x, grad_y, grad_z):
        stiffness = stiffness + gradient.T @ (quad_weights[:, None] * gradient)
    return (interp.astype(np.float32), stiffness.astype(np.float32))


def round_up(value, step):
    return -(-value // step) * step


def split(value):
    high = value.astype(jnp.bfloat16)
    low = (value - high.astype(jnp.float32)).astype(jnp.bfloat16)
    return high, low


def kernel(
    shape,
    interp,
    right_ref,
    reaction_ref,
    cells_ref,
    level_ref,
    masters_ref,
    rows_ref,
    lists_ref,
    stiff_ref,
    solution_ref,
    residual_ref,
    table,
    onehot,
    lane_of,
    row_of,
    weights,
    cell_buf,
    acc,
    out_src,
    out_dst,
    back_src,
    back_dst,
    part,
    first_buf,
    mid_part,
    second_buf,
    out_send,
    out_recv,
    back_send,
    back_recv,
    first_send,
    first_recv,
    second_send,
    second_recv,
):
    nx, ny = shape
    count = nx * ny
    me = lax.axis_index("gx") * ny + lax.axis_index("gy")

    def place(rank):
        return (lax.div(rank, ny), lax.rem(rank, ny))

    blocks, listed = lists_ref.shape
    half = blocks // 2
    offsets = [j + 1 for j in range(half)] + [-(j + 1) for j in range(half)]
    own_rows = right_ref.shape[0]
    block_rows = listed // LANES
    ghost_rows = blocks * block_rows
    local_rows = own_rows + ghost_rows
    con_rows = rows_ref.shape[0]
    all_rows = round_up(local_rows + con_rows, 16)
    nodes = masters_ref.shape[0]
    points = cells_ref.shape[0]
    cell_rows = round_up(points, 8)
    cell_groups = cell_rows // 8
    list_groups = ghost_rows // 8
    list_base = cell_groups
    con_base = cell_groups + list_groups
    near = 1
    while near * near < count:
        near *= 2
    far = count // near
    near_id, far_id = lax.rem(me, near), lax.div(me, near)

    def near_peer(step):
        return far_id * near + lax.rem(near_id + step, near)

    def far_peer(step):
        return lax.rem(far_id + step, far) * near + near_id

    def ring_peer(offset):
        return lax.rem(me + offset + count, count)

    barrier = pltpu.get_barrier_semaphore()
    peers = [ring_peer(offset) for offset in offsets]
    peers += [near_peer(step) for step in range(1, near)]
    peers += [far_peer(step) for step in range(1, far)]
    for peer in peers:
        pl.semaphore_signal(barrier, inc=1, device_id=place(peer), device_id_type=MESH)

    lane_of[...] = jnp.zeros_like(lane_of)
    row_of[...] = jnp.full_like(row_of, -1)

    def put(at, slots):
        size = slots.shape[0]
        lane_of[at : at + size, :] = lax.rem(slots, LANES)
        row_of[at : at + size, :] = lax.div(slots, LANES)

    put(0, cells_ref[...])
    for j in range(blocks):
        for q in range(block_rows):
            put(list_base * 8 + j * block_rows + q, lists_ref[j : j + 1, q * LANES : (q + 1) * LANES])
    weights[...] = jnp.zeros_like(weights)
    for h in range(con_rows):
        put((con_base + h) * 8, masters_ref[:, h * LANES : (h + 1) * LANES])
        chosen = rows_ref[h : h + 1, :]
        for k in range(nodes):
            weight = jnp.zeros((1, LANES), jnp.float32)
            for t in range(interp.shape[0]):
                weight = jnp.where(chosen == t, float(interp[t, k]), weight)
            weights[h * 8 + k : h * 8 + k + 1, :] = weight

    lane_iota = lax.broadcasted_iota(jnp.int32, (LANES, LANES), 0)

    def build(g, carry):
        lanes = lane_of[pl.ds(pl.multiple_of(g * 8, 8), 8), :]
        for i in range(8):
            hit = jnp.where(lanes[i : i + 1, :] == lane_iota, 1.0, 0.0)
            onehot[g, :, i * LANES : (i + 1) * LANES] = hit.astype(jnp.bfloat16)
        return carry

    lax.fori_loop(0, onehot.shape[0], build, 0)
    table[...] = jnp.zeros_like(table)
    cell_buf[...] = jnp.zeros_like(cell_buf)
    scale = jnp.exp2(-level_ref[...].astype(jnp.float32))

    iota8 = lax.broadcasted_iota(jnp.int32, (8, LANES), 0)

    def gather(g, depth):
        hits = onehot[g]
        spread = jnp.dot(
            table[0:depth, :],
            jnp.concatenate([hits, hits], axis=0),
            preferred_element_type=jnp.float32,
        )
        rows = row_of[pl.ds(pl.multiple_of(g * 8, 8), 8), :]
        found = []
        for i in range(8):
            wanted = jnp.broadcast_to(rows[i : i + 1, :], (8, LANES)) - iota8
            picked = jnp.zeros((8, LANES), jnp.float32)
            for k in range(depth // 8):
                block = spread[8 * k : 8 * k + 8, i * LANES : (i + 1) * LANES]
                picked = jnp.where(wanted == 8 * k, block, picked)
            found.append(jnp.sum(picked, axis=0, keepdims=True))
        return jnp.concatenate(found, axis=0)

    def scatter(g, values, depth):
        rows = row_of[pl.ds(pl.multiple_of(g * 8, 8), 8), :]
        high = values.astype(jnp.bfloat16).astype(jnp.float32)
        low = values - high
        row_iota = lax.broadcasted_iota(jnp.int32, (depth, LANES), 0)
        columns = []
        for i in range(8):
            hit = rows[i : i + 1, :] == row_iota
            upper = jnp.where(hit, high[i : i + 1, :], 0.0).astype(jnp.bfloat16)
            lower = jnp.where(hit, low[i : i + 1, :], 0.0).astype(jnp.bfloat16)
            columns.append(jnp.concatenate([upper, lower], axis=0))
        placed = jnp.concatenate(columns, axis=1)
        return lax.dot_general(
            placed, onehot[g], (((1,), (1,)), ((), ())), preferred_element_type=jnp.float32
        )

    def store(at, value):
        high, low = split(value)
        size = value.shape[0]
        table[at : at + size, 0:LANES] = high
        table[at : at + size, LANES : 2 * LANES] = low

    def out_copy(turn, j):
        return pltpu.make_async_remote_copy(
            src_ref=out_src.at[turn, j],
            dst_ref=out_dst.at[turn, j],
            send_sem=out_send.at[turn, j],
            recv_sem=out_recv.at[turn, j],
            device_id=place(ring_peer(offsets[j])),
            device_id_type=MESH,
        )

    def back_copy(turn, j):
        return pltpu.make_async_remote_copy(
            src_ref=back_src.at[turn, j],
            dst_ref=back_dst.at[turn, j],
            send_sem=back_send.at[turn, j],
            recv_sem=back_recv.at[turn, j],
            device_id=place(ring_peer(-offsets[j])),
            device_id_type=MESH,
        )

    def near_copy(turn, step):
        return pltpu.make_async_remote_copy(
            src_ref=part.at[turn],
            dst_ref=first_buf.at[turn, near_id],
            send_sem=first_send.at[turn, step],
            recv_sem=first_recv.at[turn, step],
            device_id=place(near_peer(step)),
            device_id_type=MESH,
        )

    def far_copy(turn, step):
        return pltpu.make_async_remote_copy(
            src_ref=mid_part.at[turn],
            dst_ref=second_buf.at[turn, far_id],
            send_sem=second_send.at[turn, step],
            recv_sem=second_recv.at[turn, step],
            device_id=place(far_peer(step)),
            device_id_type=MESH,
        )

    def received(ref, turn, signs):
        rows = []
        for j in range(blocks):
            other = me + signs * offsets[j]
            inside = jnp.logical_and(other >= 0, other < count)
            rows.append(jnp.where(inside, ref[turn, j], 0.0))
        return jnp.concatenate(rows, axis=0)

    def apply(turn, vector, middle):
        store(0, vector)
        per_group = 8 // block_rows
        for q in range(list_groups):
            found = gather(list_base + q, own_rows)
            for r in range(per_group):
                j = q * per_group + r
                out_src[turn, j] = found[r * block_rows : (r + 1) * block_rows]
        for j in range(blocks):
            out_copy(turn, j).start()
        for j in range(blocks):
            out_copy(turn, j).wait()
        middle()
        store(own_rows, received(out_dst, turn, -1))
        resolved = []
        for h in range(con_rows):
            found = gather(con_base + h, local_rows)
            resolved.append(jnp.sum(weights[8 * h : 8 * h + 8, :] * found, axis=0, keepdims=True))
        spare = all_rows - local_rows - con_rows
        resolved.append(jnp.zeros((spare, LANES), jnp.float32))
        store(local_rows, jnp.concatenate(resolved, axis=0))

        def take(g, carry):
            cell_buf[pl.ds(pl.multiple_of(g * 8, 8), 8), :] = gather(g, all_rows)
            return carry

        lax.fori_loop(0, cell_groups, take, 0)
        contrib = jnp.dot(
            stiff_ref[...],
            cell_buf[...],
            precision=lax.Precision.HIGHEST,
            preferred_element_type=jnp.float32,
        )
        cell_buf[...] = contrib * scale
        acc[...] = jnp.zeros_like(acc)

        def give(g, carry):
            values = cell_buf[pl.ds(pl.multiple_of(g * 8, 8), 8), :]
            acc[...] += scatter(g, values, all_rows)
            return carry

        lax.fori_loop(0, cell_groups, give, 0)
        summed = acc[0:all_rows, :] + acc[all_rows : 2 * all_rows, :]
        spread = summed[0:local_rows]
        for h in range(con_rows):
            at = local_rows + h
            values = weights[8 * h : 8 * h + 8, :] * summed[at : at + 1]
            both = scatter(con_base + h, values, local_rows)
            spread = spread + both[0:local_rows] + both[local_rows : 2 * local_rows]
        for j in range(blocks):
            at = own_rows + j * block_rows
            back_src[turn, j] = spread[at : at + block_rows]
        for j in range(blocks):
            back_copy(turn, j).start()
        result = spread[0:own_rows] + reaction_ref[...] * vector
        for j in range(blocks):
            back_copy(turn, j).wait()
        values = received(back_dst, turn, 1)
        for q in range(list_groups):
            both = scatter(list_base + q, values[8 * q : 8 * q + 8], own_rows)
            result = result + both[0:own_rows] + both[own_rows : 2 * own_rows]
        return result

    def sums_start(turn, vector, applied):
        mine = jnp.concatenate(
            [
                jnp.sum(vector * vector, axis=0, keepdims=True),
                jnp.sum(vector * applied, axis=0, keepdims=True),
            ],
            axis=0,
        )
        part[turn] = mine
        first_buf[turn, near_id] = mine
        for step in range(1, near):
            near_copy(turn, step).start()

    def sums_middle(turn):
        for step in range(1, near):
            near_copy(turn, step).wait()
        mine = first_buf[turn, 0]
        for k in range(1, near):
            mine = mine + first_buf[turn, k]
        mid_part[turn] = mine
        second_buf[turn, far_id] = mine
        for step in range(1, far):
            far_copy(turn, step).start()

    def sums_end(turn):
        for step in range(1, far):
            far_copy(turn, step).wait()
        total = second_buf[turn, 0]
        for k in range(1, far):
            total = total + second_buf[turn, k]
        total = jnp.sum(total, axis=1, keepdims=True)
        return total[0:1], total[1:2]

    pl.semaphore_wait(barrier, len(peers))

    residual = right_ref[...]
    applied = apply(0, residual, lambda: None)
    answer = direction = applied_dir = twice_dir = None
    norm_before = step_before = None
    for turn in range(ITERS):
        sums_start(turn, residual, applied)
        last = turn + 1 == ITERS
        if last:
            sums_middle(turn)
        else:
            twice = apply(turn + 1, applied, functools.partial(sums_middle, turn))
        norm, product = sums_end(turn)
        if turn == 0:
            step_size = norm / product
            direction, applied_dir = residual, applied
            if not last:
                twice_dir = twice
            answer = step_size * direction
        else:
            ratio = norm / norm_before
            step_size = norm / (product - ratio * norm / step_before)
            direction = residual + ratio * direction
            applied_dir = applied + ratio * applied_dir
            if not last:
                twice_dir = twice + ratio * twice_dir
            answer = answer + step_size * direction
        residual = residual - step_size * applied_dir
        if not last:
            applied = applied - step_size * twice_dir
        norm_before, step_before = norm, step_size
    solution_ref[...] = answer
    residual_ref[...] = residual


def on_device(shape, right_side, reaction, cell_slots, cell_level, con_masters, con_rows, send_lists):
    interp, stiffness = tables()
    own = right_side.shape[0]
    own_rows = own // LANES
    blocks, listed = send_lists.shape
    block_rows = listed // LANES
    con_tiles = con_rows.shape[0] // LANES
    points = cell_slots.shape[0]
    cell_rows = round_up(points, 8)
    all_rows = round_up(own_rows + blocks * block_rows + con_tiles, 16)
    groups = cell_rows // 8 + blocks * block_rows // 8 + con_tiles
    padded = np.zeros((cell_rows, cell_rows), np.float32)
    padded[:points, :points] = stiffness
    count = shape[0] * shape[1]
    near = 1
    while near * near < count:
        near *= 2
    far = count // near
    exchange = pltpu.VMEM((ITERS, blocks, block_rows, LANES), jnp.float32)
    tile = jax.ShapeDtypeStruct((own_rows, LANES), jnp.float32)
    answer, residual = pl.pallas_call(
        functools.partial(kernel, shape, interp),
        out_shape=(tile, tile),
        in_specs=[pl.BlockSpec(memory_space=pltpu.VMEM)] * 8,
        out_specs=(pl.BlockSpec(memory_space=pltpu.VMEM),) * 2,
        scratch_shapes=[
            pltpu.VMEM((all_rows, 2 * LANES), jnp.bfloat16),
            pltpu.VMEM((groups, LANES, 8 * LANES), jnp.bfloat16),
            pltpu.VMEM((groups * 8, LANES), jnp.int32),
            pltpu.VMEM((groups * 8, LANES), jnp.int32),
            pltpu.VMEM((con_tiles * 8, LANES), jnp.float32),
            pltpu.VMEM((cell_rows, LANES), jnp.float32),
            pltpu.VMEM((2 * all_rows, LANES), jnp.float32),
            exchange,
            exchange,
            exchange,
            exchange,
            pltpu.VMEM((ITERS, 2, LANES), jnp.float32),
            pltpu.VMEM((ITERS, near, 2, LANES), jnp.float32),
            pltpu.VMEM((ITERS, 2, LANES), jnp.float32),
            pltpu.VMEM((ITERS, far, 2, LANES), jnp.float32),
            pltpu.SemaphoreType.DMA((ITERS, blocks)),
            pltpu.SemaphoreType.DMA((ITERS, blocks)),
            pltpu.SemaphoreType.DMA((ITERS, blocks)),
            pltpu.SemaphoreType.DMA((ITERS, blocks)),
            pltpu.SemaphoreType.DMA((ITERS, near)),
            pltpu.SemaphoreType.DMA((ITERS, near)),
            pltpu.SemaphoreType.DMA((ITERS, far)),
            pltpu.SemaphoreType.DMA((ITERS, far)),
        ],
        compiler_params=pltpu.CompilerParams(
            collective_id=0, has_side_effects=True, vmem_limit_bytes=40 * 1024 * 1024
        ),
    )(
        right_side.reshape(own_rows, LANES),
        reaction.reshape(own_rows, LANES),
        cell_slots,
        cell_level.reshape(1, -1),
        con_masters,
        con_rows.reshape(con_tiles, LANES),
        send_lists,
        jnp.asarray(padded),
    )
    return (answer.reshape(own), residual.reshape(own))


def solution(mesh):
    placed = (
        P(("gx", "gy")),
        P(("gx", "gy")),
        P(None, ("gx", "gy")),
        P(("gx", "gy")),
        P(None, ("gx", "gy")),
        P(("gx", "gy")),
        P(None, ("gx", "gy")),
    )
    return jax.shard_map(
        functools.partial(on_device, (mesh.shape["gx"], mesh.shape["gy"])),
        mesh=mesh,
        in_specs=placed,
        out_specs=(P(("gx", "gy")), P(("gx", "gy"))),
        check_vma=False,
    )
```

time: 998 us -> 80.9 us (0.08)
  other arithmetic: 349 us -> 0 us
  local copies, waits for them, and re-layouts: 339 us -> 6.51 us
  blocking collectives: 148 us -> 0 us
  starting transfers between devices: 136 us -> 0 us
  Pallas kernels: 0 us -> 73.3 us
  waiting for transfers between devices: 11.3 us -> 0 us
  between operations: 11.6 us -> 0.66 us
    scatter-add x9 -> x0, other arithmetic: 345 us -> none  [the longest x3 255 us: local_apply(): jnp.zeros(full_list.shape, jnp.float32).at[slot_map.reshape(-1)]]
    gather x12 -> x0, local copies, waits for them, and re-layouts: 337 us -> none  [the longest x3 247 us: local_apply(): cell_values = full_list[slot_map]]
    psum x3 -> x0, blocking collectives: 148 us -> none  [paired_sums(): lax.psum((jnp.sum(vector * vector), jnp.sum(vector * applied)), ('gx', 'g...]
    ppermute x48 -> x0, starting transfers between devices: 136 us -> none  [shifted(): lax.ppermute(value, axis, [(source, source + steps) for source in range(i...]
    pallas_call x0 -> x1, Pallas kernels: none -> 73.3 us  [on_device(): pl.pallas_call(functools.partial(kernel, shape, interp), out_shape=(tile,...]
    ppermute x48 -> x0, waiting for transfers between devices: 11.3 us -> none  [shifted(): lax.ppermute(value, axis, [(source, source + steps) for source in range(i...]
  transfers between devices with their start and end apart: 48 -> 0, of which waited for: 12 -> 0; matrix products, arithmetic and copies ran while one was open for 0% -> 0% of each run, Pallas kernels for 0% -> 0%
where the time goes in v1:
time: 80.9 us; the launch traced here: 80.4 us
  Pallas kernels  73.3 us (91%)
  local copies, waits for them, and re-layouts  6.51 us (8%)
    pallas_call x1, Pallas kernels, on_device(): pl.pallas_call(functools.partial(kernel, shape, interp), out_shape=(tile,...  73.3 us
    unnamed x18, local copies, waits for them, and re-layouts  6.51 us

profile of v1, /device:TPU:0, one launch (start us, length us, event | category | flops | bytes accessed | tf_op | source)
XLA Modules:
  0.0 80.4 jit_solution(12530957409166077334)
XLA Ops:
  0.6 0.0 copy-start.6
  0.6 0.0 copy-start.7
  0.7 0.7 copy-done.6
  1.3 0.0 copy-done.7
  1.3 0.0 copy-start
  1.3 0.8 %copy-done = s32[125,128]{1,0:T(8,128)S(1)} copy-done((s32[125,128]{1,0:T(8,128)S(1)}, s32[125,128]{1,0:T(8,128)}, u32[]{:S(2)}) %copy-start) | copy-done | bytes 64024
  2.2 0.0 copy-start.1
  2.2 0.8 %copy-done.1 = f32[128,128]{1,0:T(8,128)S(1)} copy-done((f32[128,128]{1,0:T(8,128)S(1)}, f32[128,128]{1,0:T(8,128)}, u32[]{:S(2)}) %copy-start.1) | copy-done | bytes 65560
  3.0 0.0 copy-start.2
  3.0 0.8 copy-done.2
  3.8 0.0 copy-start.3
  3.8 0.8 copy-done.3
  4.5 0.0 copy-start.4
  4.5 0.7 copy-done.4
  5.2 0.0 copy-start.5
  5.2 0.7 copy-done.5
  5.9 73.3 %shard_map.95 = (f32[64,128]{1,0:T(8,128)S(1)}, f32[64,128]{1,0:T(8,128)S(1)}) custom-call(f32[64,128]{1,0:T(8,128)S(1)} %bitcast.6, f32[64,128]{1,0:T(8,128)S(1)} %bitcast.7, s32[125,128]{1,0:T(8,128)S(1)} %copy-done, s32[1,128]{1,0:T(1,128)S(1)} %bitcast.11, s32[5,256]{1,0:T(8,128)S(1)} %copy-done.5, s32[2,128]{1,0:T(2,128)S(1)} %bitcast.10, ...), custom_call_target="tpu_custom_call" | custom-call | tf_op jit(solution)/shard_map/pallas_call | solution.py:438
  79.2 0.6 copy.12
  79.8 0.6 copy.13
Async XLA Ops:
  0.6 0.7 copy-start.6
  0.6 0.7 copy-start.7
  1.3 0.8 %copy-start = (s32[125,128]{1,0:T(8,128)S(1)}, s32[125,128]{1,0:T(8,128)}, u32[]{:S(2)}) copy-start(s32[125,128]{1,0:T(8,128)} %cells_ref.1) | copy-start | bytes 192004
  2.2 0.8 %copy-start.1 = (f32[128,128]{1,0:T(8,128)S(1)}, f32[128,128]{1,0:T(8,128)}, u32[]{:S(2)}) copy-start(f32[128,128]{1,0:T(8,128)} %constant.2.clone.stiff_ref) | copy-start | bytes 196612
  3.0 0.8 copy-start.2
  3.8 0.8 copy-start.3
  4.5 0.7 copy-start.4
  5.2 0.7 copy-start.5

commit v2 on v1

--- a/solution.py
+++ b/solution.py
@@ -10,6 +10,8 @@
 
 ITERS = 3
 LANES = 128
+SUMS = 4
+ROUNDS = 2
 MESH = pl.DeviceIdType.MESH
 
 
@@ -78,23 +80,23 @@
 def kernel(
     shape,
     interp,
-    right_ref,
-    reaction_ref,
-    cells_ref,
-    level_ref,
-    masters_ref,
-    rows_ref,
-    lists_ref,
-    stiff_ref,
-    solution_ref,
-    residual_ref,
-    table,
+    *refs,
+):
+    inputs, refs = refs[:8], refs[8:]
+    solution_ref, residual_ref = refs[:2]
+    staged, refs = refs[2:10], refs[10:]
+    right_ref, reaction_ref, cells_ref, level_ref, masters_ref, rows_ref, lists_ref, stiff_ref = staged
+    (
+    load_sem,
+    own_table,
+    ghost_table,
     onehot,
     lane_of,
     row_of,
     weights,
     cell_buf,
-    acc,
+    own_acc,
+    ghost_acc,
     out_src,
     out_dst,
     back_src,
@@ -111,7 +113,13 @@
     first_recv,
     second_send,
     second_recv,
-):
+    ) = refs
+    loads = [
+        pltpu.make_async_copy(source, target, load_sem.at[i])
+        for i, (source, target) in enumerate(zip(inputs, staged))
+    ]
+    for load in loads:
+        load.start()
     nx, ny = shape
     count = nx * ny
     me = lax.axis_index("gx") * ny + lax.axis_index("gy")
@@ -127,7 +135,7 @@
     ghost_rows = blocks * block_rows
     local_rows = own_rows + ghost_rows
     con_rows = rows_ref.shape[0]
-    all_rows = round_up(local_rows + con_rows, 16)
+    far_rows = round_up(ghost_rows + con_rows, 16)
     nodes = masters_ref.shape[0]
     points = cells_ref.shape[0]
     cell_rows = round_up(points, 8)
@@ -157,6 +165,8 @@
     for peer in peers:
         pl.semaphore_signal(barrier, inc=1, device_id=place(peer), device_id_type=MESH)
 
+    for load in loads:
+        load.wait()
     lane_of[...] = jnp.zeros_like(lane_of)
     row_of[...] = jnp.full_like(row_of, -1)
 
@@ -189,32 +199,32 @@
         return carry
 
     lax.fori_loop(0, onehot.shape[0], build, 0)
-    table[...] = jnp.zeros_like(table)
     cell_buf[...] = jnp.zeros_like(cell_buf)
     scale = jnp.exp2(-level_ref[...].astype(jnp.float32))
 
     iota8 = lax.broadcasted_iota(jnp.int32, (8, LANES), 0)
 
-    def gather(g, depth):
-        hits = onehot[g]
-        spread = jnp.dot(
-            table[0:depth, :],
-            jnp.concatenate([hits, hits], axis=0),
-            preferred_element_type=jnp.float32,
-        )
-        rows = row_of[pl.ds(pl.multiple_of(g * 8, 8), 8), :]
+    def gather(g, table, base, depth):
+        stacked = table.shape[0] // 2
+        pieces = [table[0:depth, :], table[stacked : stacked + depth, :]]
+        left = table[...] if depth == stacked else jnp.concatenate(pieces, axis=0)
+        spread = jnp.dot(left, onehot[g], preferred_element_type=jnp.float32)
+        rows = row_of[pl.ds(pl.multiple_of(g * 8, 8), 8), :] - base
         found = []
         for i in range(8):
             wanted = jnp.broadcast_to(rows[i : i + 1, :], (8, LANES)) - iota8
-            picked = jnp.zeros((8, LANES), jnp.float32)
+            high = jnp.zeros((8, LANES), jnp.float32)
+            low = high
             for k in range(depth // 8):
-                block = spread[8 * k : 8 * k + 8, i * LANES : (i + 1) * LANES]
-                picked = jnp.where(wanted == 8 * k, block, picked)
-            found.append(jnp.sum(picked, axis=0, keepdims=True))
+                hit = wanted == 8 * k
+                at, cols = 8 * k, slice(i * LANES, (i + 1) * LANES)
+                high = jnp.where(hit, spread[at : at + 8, cols], high)
+                low = jnp.where(hit, spread[depth + at : depth + at + 8, cols], low)
+            found.append(jnp.sum(high + low, axis=0, keepdims=True))
         return jnp.concatenate(found, axis=0)
 
-    def scatter(g, values, depth):
-        rows = row_of[pl.ds(pl.multiple_of(g * 8, 8), 8), :]
+    def scatter(g, values, base, depth):
+        rows = row_of[pl.ds(pl.multiple_of(g * 8, 8), 8), :] - base
         high = values.astype(jnp.bfloat16).astype(jnp.float32)
         low = values - high
         row_iota = lax.broadcasted_iota(jnp.int32, (depth, LANES), 0)
@@ -229,11 +239,15 @@
             placed, onehot[g], (((1,), (1,)), ((), ())), preferred_element_type=jnp.float32
         )
 
-    def store(at, value):
+    def folded(both):
+        depth = both.shape[0] // 2
+        return both[0:depth] + both[depth : 2 * depth]
+
+    def store(table, value):
         high, low = split(value)
         size = value.shape[0]
-        table[at : at + size, 0:LANES] = high
-        table[at : at + size, LANES : 2 * LANES] = low
+        table[0:size, :] = high
+        table[size : 2 * size, :] = low
 
     def out_copy(turn, j):
         return pltpu.make_async_remote_copy(
@@ -283,77 +297,98 @@
             rows.append(jnp.where(inside, ref[turn, j], 0.0))
         return jnp.concatenate(rows, axis=0)
 
-    def apply(turn, vector, middle):
-        store(0, vector)
+    def group(g):
+        return pl.ds(pl.multiple_of(g * 8, 8), 8)
+
+    def apply(turn, vector, begin, middle):
+        store(own_table, vector)
         per_group = 8 // block_rows
         for q in range(list_groups):
-            found = gather(list_base + q, own_rows)
+            found = gather(list_base + q, own_table, 0, own_rows)
             for r in range(per_group):
                 j = q * per_group + r
                 out_src[turn, j] = found[r * block_rows : (r + 1) * block_rows]
+        if turn == 0:
+            pl.semaphore_wait(barrier, len(peers))
         for j in range(blocks):
             out_copy(turn, j).start()
+
+        def take_own(g, carry):
+            cell_buf[group(g), :] = gather(g, own_table, 0, own_rows)
+            return carry
+
+        lax.fori_loop(0, cell_groups, take_own, 0)
+        con_own = [gather(con_base + h, own_table, 0, own_rows) for h in range(con_rows)]
         for j in range(blocks):
             out_copy(turn, j).wait()
-        middle()
-        store(own_rows, received(out_dst, turn, -1))
+        ghosts = received(out_dst, turn, -1)
+        padding = jnp.zeros((far_rows - ghost_rows, LANES), jnp.float32)
+        store(ghost_table, jnp.concatenate([ghosts, padding], axis=0))
         resolved = []
         for h in range(con_rows):
-            found = gather(con_base + h, local_rows)
+            found = con_own[h] + gather(con_base + h, ghost_table, own_rows, ghost_rows)
             resolved.append(jnp.sum(weights[8 * h : 8 * h + 8, :] * found, axis=0, keepdims=True))
-        spare = all_rows - local_rows - con_rows
-        resolved.append(jnp.zeros((spare, LANES), jnp.float32))
-        store(local_rows, jnp.concatenate(resolved, axis=0))
-
-        def take(g, carry):
-            cell_buf[pl.ds(pl.multiple_of(g * 8, 8), 8), :] = gather(g, all_rows)
+        resolved.append(jnp.zeros((far_rows - ghost_rows - con_rows, LANES), jnp.float32))
+        store(ghost_table, jnp.concatenate([ghosts] + resolved, axis=0))
+
+        def take_far(g, carry):
+            cell_buf[group(g), :] += gather(g, ghost_table, own_rows, far_rows)
             return carry
 
-        lax.fori_loop(0, cell_groups, take, 0)
-        contrib = jnp.dot(
+        lax.fori_loop(0, cell_groups, take_far, 0)
+        nodal = cell_buf[...]
+        contrib = scale * jnp.dot(
             stiff_ref[...],
-            cell_buf[...],
+            nodal,
             precision=lax.Precision.HIGHEST,
             preferred_element_type=jnp.float32,
         )
-        cell_buf[...] = contrib * scale
-        acc[...] = jnp.zeros_like(acc)
-
-        def give(g, carry):
-            values = cell_buf[pl.ds(pl.multiple_of(g * 8, 8), 8), :]
-            acc[...] += scatter(g, values, all_rows)
+        cell_buf[...] = contrib
+        weighted = reaction_ref[...] * vector
+        energy = jnp.sum(nodal * contrib, axis=0, keepdims=True)
+        energy = energy + jnp.sum(weighted * vector, axis=0, keepdims=True)
+        begin(energy)
+        ghost_acc[...] = jnp.zeros_like(ghost_acc)
+
+        def give_far(g, carry):
+            ghost_acc[...] += scatter(g, cell_buf[group(g), :], own_rows, far_rows)
             return carry
 
-        lax.fori_loop(0, cell_groups, give, 0)
-        summed = acc[0:all_rows, :] + acc[all_rows : 2 * all_rows, :]
-        spread = summed[0:local_rows]
+        lax.fori_loop(0, cell_groups, give_far, 0)
+        summed = folded(ghost_acc[...])
+        spread = summed[0:ghost_rows]
+        shares = []
         for h in range(con_rows):
-            at = local_rows + h
-            values = weights[8 * h : 8 * h + 8, :] * summed[at : at + 1]
-            both = scatter(con_base + h, values, local_rows)
-            spread = spread + both[0:local_rows] + both[local_rows : 2 * local_rows]
+            at = ghost_rows + h
+            shares.append(weights[8 * h : 8 * h + 8, :] * summed[at : at + 1])
+            spread = spread + folded(scatter(con_base + h, shares[h], own_rows, ghost_rows))
         for j in range(blocks):
-            at = own_rows + j * block_rows
-            back_src[turn, j] = spread[at : at + block_rows]
+            back_src[turn, j] = spread[j * block_rows : (j + 1) * block_rows]
         for j in range(blocks):
             back_copy(turn, j).start()
-        result = spread[0:own_rows] + reaction_ref[...] * vector
+        middle()
+        own_acc[...] = jnp.zeros_like(own_acc)
+
+        def give_own(g, carry):
+            own_acc[...] += scatter(g, cell_buf[group(g), :], 0, own_rows)
+            return carry
+
+        lax.fori_loop(0, cell_groups, give_own, 0)
+        both = own_acc[...]
+        for h in range(con_rows):
+            both = both + scatter(con_base + h, shares[h], 0, own_rows)
         for j in range(blocks):
             back_copy(turn, j).wait()
         values = received(back_dst, turn, 1)
         for q in range(list_groups):
-            both = scatter(list_base + q, values[8 * q : 8 * q + 8], own_rows)
-            result = result + both[0:own_rows] + both[own_rows : 2 * own_rows]
-        return result
-
-    def sums_start(turn, vector, applied):
-        mine = jnp.concatenate(
-            [
-                jnp.sum(vector * vector, axis=0, keepdims=True),
-                jnp.sum(vector * applied, axis=0, keepdims=True),
-            ],
-            axis=0,
-        )
+            both = both + scatter(list_base + q, values[8 * q : 8 * q + 8], 0, own_rows)
+        return folded(both) + weighted
+
+    def dot(one, two):
+        return jnp.sum(one * two, axis=0, keepdims=True)
+
+    def sums_start(turn, parts):
+        mine = jnp.concatenate(parts, axis=0)
         part[turn] = mine
         first_buf[turn, near_id] = mine
         for step in range(1, near):
@@ -377,42 +412,42 @@
         for k in range(1, far):
             total = total + second_buf[turn, k]
         total = jnp.sum(total, axis=1, keepdims=True)
-        return total[0:1], total[1:2]
-
-    pl.semaphore_wait(barrier, len(peers))
-
-    residual = right_ref[...]
-    applied = apply(0, residual, lambda: None)
-    answer = direction = applied_dir = twice_dir = None
-    norm_before = step_before = None
-    for turn in range(ITERS):
-        sums_start(turn, residual, applied)
-        last = turn + 1 == ITERS
-        if last:
-            sums_middle(turn)
-        else:
-            twice = apply(turn + 1, applied, functools.partial(sums_middle, turn))
-        norm, product = sums_end(turn)
-        if turn == 0:
-            step_size = norm / product
-            direction, applied_dir = residual, applied
-            if not last:
-                twice_dir = twice
-            answer = step_size * direction
-        else:
-            ratio = norm / norm_before
-            step_size = norm / (product - ratio * norm / step_before)
-            direction = residual + ratio * direction
-            applied_dir = applied + ratio * applied_dir
-            if not last:
-                twice_dir = twice + ratio * twice_dir
-            answer = answer + step_size * direction
-        residual = residual - step_size * applied_dir
-        if not last:
-            applied = applied - step_size * twice_dir
-        norm_before, step_before = norm, step_size
-    solution_ref[...] = answer
-    residual_ref[...] = residual
+        return [total[k : k + 1] for k in range(SUMS)]
+
+    start = right_ref[...]
+    first = apply(0, start, lambda energy: None, lambda: None)
+    known = [dot(start, start), dot(start, first), dot(first, first)]
+    second = apply(
+        1,
+        first,
+        lambda energy: sums_start(0, known + [energy]),
+        lambda: sums_middle(0),
+    )
+    m0, m1, m2, m3 = sums_end(0)
+    step0 = m0 / m1
+    norm1 = m0 - 2.0 * step0 * m1 + step0 * step0 * m2
+    product1 = m1 - 2.0 * step0 * m2 + step0 * step0 * m3
+    ratio1 = norm1 / m0
+    step1 = norm1 / (product1 - ratio1 * norm1 / step0)
+    residual = start - step0 * first
+    applied = first - step0 * second
+    direction = residual + ratio1 * start
+    applied_dir = applied + ratio1 * first
+    answer = step0 * start + step1 * direction
+    residual = residual - step1 * applied_dir
+    zero = jnp.zeros((1, LANES), jnp.float32)
+    square = dot(residual, residual)
+    applied = apply(
+        2,
+        residual,
+        lambda energy: sums_start(1, [square, energy, zero, zero]),
+        lambda: sums_middle(1),
+    )
+    norm2, product2, unused_a, unused_b = sums_end(1)
+    ratio2 = norm2 / norm1
+    step2 = norm2 / (product2 - ratio2 * norm2 / step1)
+    solution_ref[...] = answer + step2 * (residual + ratio2 * direction)
+    residual_ref[...] = residual - step2 * (applied + ratio2 * applied_dir)
 
 
 def on_device(shape, right_side, reaction, cell_slots, cell_level, con_masters, con_rows, send_lists):
@@ -424,7 +459,7 @@
     con_tiles = con_rows.shape[0] // LANES
     points = cell_slots.shape[0]
     cell_rows = round_up(points, 8)
-    all_rows = round_up(own_rows + blocks * block_rows + con_tiles, 16)
+    far_rows = round_up(blocks * block_rows + con_tiles, 16)
     groups = cell_rows // 8 + blocks * block_rows // 8 + con_tiles
     padded = np.zeros((cell_rows, cell_rows), np.float32)
     padded[:points, :points] = stiffness
@@ -433,42 +468,7 @@
     while near * near < count:
         near *= 2
     far = count // near
-    exchange = pltpu.VMEM((ITERS, blocks, block_rows, LANES), jnp.float32)
-    tile = jax.ShapeDtypeStruct((own_rows, LANES), jnp.float32)
-    answer, residual = pl.pallas_call(
-        functools.partial(kernel, shape, interp),
-        out_shape=(tile, tile),
-        in_specs=[pl.BlockSpec(memory_space=pltpu.VMEM)] * 8,
-        out_specs=(pl.BlockSpec(memory_space=pltpu.VMEM),) * 2,
-        scratch_shapes=[
-            pltpu.VMEM((all_rows, 2 * LANES), jnp.bfloat16),
-            pltpu.VMEM((groups, LANES, 8 * LANES), jnp.bfloat16),
-            pltpu.VMEM((groups * 8, LANES), jnp.int32),
-            pltpu.VMEM((groups * 8, LANES), jnp.int32),
-            pltpu.VMEM((con_tiles * 8, LANES), jnp.float32),
-            pltpu.VMEM((cell_rows, LANES), jnp.float32),
-            pltpu.VMEM((2 * all_rows, LANES), jnp.float32),
-            exchange,
-            exchange,
-            exchange,
-            exchange,
-            pltpu.VMEM((ITERS, 2, LANES), jnp.float32),
-            pltpu.VMEM((ITERS, near, 2, LANES), jnp.float32),
-            pltpu.VMEM((ITERS, 2, LANES), jnp.float32),
-            pltpu.VMEM((ITERS, far, 2, LANES), jnp.float32),
-            pltpu.SemaphoreType.DMA((ITERS, blocks)),
-            pltpu.SemaphoreType.DMA((ITERS, blocks)),
-            pltpu.SemaphoreType.DMA((ITERS, blocks)),
-            pltpu.SemaphoreType.DMA((ITERS, blocks)),
-            pltpu.SemaphoreType.DMA((ITERS, near)),
-            pltpu.SemaphoreType.DMA((ITERS, near)),
-            pltpu.SemaphoreType.DMA((ITERS, far)),
-            pltpu.SemaphoreType.DMA((ITERS, far)),
-        ],
-        compiler_params=pltpu.CompilerParams(
-            collective_id=0, has_side_effects=True, vmem_limit_bytes=40 * 1024 * 1024
-        ),
-    )(
+    operands = [
         right_side.reshape(own_rows, LANES),
         reaction.reshape(own_rows, LANES),
         cell_slots,
@@ -477,7 +477,47 @@
         con_rows.reshape(con_tiles, LANES),
         send_lists,
         jnp.asarray(padded),
-    )
+    ]
+    exchange = pltpu.VMEM((ITERS, blocks, block_rows, LANES), jnp.float32)
+    tile = jax.ShapeDtypeStruct((own_rows, LANES), jnp.float32)
+    answer, residual = pl.pallas_call(
+        functools.partial(kernel, shape, interp),
+        out_shape=(tile, tile),
+        in_specs=[pl.BlockSpec(memory_space=pl.ANY)] * 8,
+        out_specs=(pl.BlockSpec(memory_space=pltpu.VMEM),) * 2,
+        scratch_shapes=[
+            *[pltpu.VMEM(value.shape, value.dtype) for value in operands],
+            pltpu.SemaphoreType.DMA((len(operands),)),
+            pltpu.VMEM((2 * own_rows, LANES), jnp.bfloat16),
+            pltpu.VMEM((2 * far_rows, LANES), jnp.bfloat16),
+            pltpu.VMEM((groups, LANES, 8 * LANES), jnp.bfloat16),
+            pltpu.VMEM((groups * 8, LANES), jnp.int32),
+            pltpu.VMEM((groups * 8, LANES), jnp.int32),
+            pltpu.VMEM((con_tiles * 8, LANES), jnp.float32),
+            pltpu.VMEM((cell_rows, LANES), jnp.float32),
+            pltpu.VMEM((2 * own_rows, LANES), jnp.float32),
+            pltpu.VMEM((2 * far_rows, LANES), jnp.float32),
+            exchange,
+            exchange,
+            exchange,
+            exchange,
+            pltpu.VMEM((ROUNDS, SUMS, LANES), jnp.float32),
+            pltpu.VMEM((ROUNDS, near, SUMS, LANES), jnp.float32),
+            pltpu.VMEM((ROUNDS, SUMS, LANES), jnp.float32),
+            pltpu.VMEM((ROUNDS, far, SUMS, LANES), jnp.float32),
+            pltpu.SemaphoreType.DMA((ITERS, blocks)),
+            pltpu.SemaphoreType.DMA((ITERS, blocks)),
+            pltpu.SemaphoreType.DMA((ITERS, blocks)),
+            pltpu.SemaphoreType.DMA((ITERS, blocks)),
+            pltpu.SemaphoreType.DMA((ROUNDS, near)),
+            pltpu.SemaphoreType.DMA((ROUNDS, near)),
+            pltpu.SemaphoreType.DMA((ROUNDS, far)),
+            pltpu.SemaphoreType.DMA((ROUNDS, far)),
+        ],
+        compiler_params=pltpu.CompilerParams(
+            collective_id=0, has_side_effects=True, vmem_limit_bytes=60 * 1024 * 1024
+        ),
+    )(*operands)
     return (answer.reshape(own), residual.reshape(own))
 
 

time: 80.9 us -> 64.2 us (0.79)
  Pallas kernels: 73.3 us -> 61.4 us
  local copies, waits for them, and re-layouts: 6.51 us -> 2 us
    pallas_call x1, Pallas kernels: 73.3 us -> 61.4 us  [on_device(): pl.pallas_call(functools.partial(kernel, shape, interp), out_shape=(tile,...]
    unnamed x18 -> x4, local copies, waits for them, and re-layouts: 6.51 us -> 2 us
where the time goes in v2:
time: 64.2 us; the launch traced here: 64 us
  Pallas kernels  61.4 us (96%)
  local copies, waits for them, and re-layouts  2 us (3%)
  between operations  0.65 us (1%)
    pallas_call x1, Pallas kernels, on_device(): pl.pallas_call(functools.partial(kernel, shape, interp), out_shape=(tile,...  61.4 us
    unnamed x4, local copies, waits for them, and re-layouts  2 us

profile of v2, /device:TPU:0, one launch (start us, length us, event | category | flops | bytes accessed | tf_op | source)
XLA Modules:
  0.0 64.0 jit_solution(2524226488605433153)
XLA Ops:
  0.6 61.4 %shard_map.95 = (f32[64,128]{1,0:T(8,128)}, f32[64,128]{1,0:T(8,128)}) custom-call(f32[64,128]{1,0:T(8,128)} %bitcast.6, f32[64,128]{1,0:T(8,128)} %bitcast.7, s32[125,128]{1,0:T(8,128)} %refs_2_.1, s32[1,128]{1,0:T(1,128)} %bitcast.11, s32[5,256]{1,0:T(8,128)} %refs_4_.1, s32[2,128]{1,0:T(2,128)} %bitcast.10, s32[8,512]{1,0:T(8,128)} %refs_6_.1, ...), custom_call_target="tpu_custom_call" | custom-call | tf_op jit(solution)/shard_map/pallas_call | solution.py:483
  62.0 0.0 copy-start
  62.0 1.4 %copy.12 = f32[8192]{0:T(1024)} copy(f32[8192]{0:T(1024)} %bitcast.9) | data formatting | bytes 65536
  63.4 0.0 copy-done
  63.4 0.6 copy.13
Async XLA Ops:
  62.0 1.4 %copy-start = (f32[64,128]{1,0:T(8,128)S(1)}, f32[64,128]{1,0:T(8,128)}, u32[]{:S(2)}) copy-start(f32[64,128]{1,0:T(8,128)} %get-tuple-element.5) | copy-start | bytes 98308

commit v3 on v2

--- a/solution.py
+++ b/solution.py
@@ -12,6 +12,7 @@
 LANES = 128
 SUMS = 4
 ROUNDS = 2
+UNROLL = 8
 MESH = pl.DeviceIdType.MESH
 
 
@@ -317,7 +318,7 @@
             cell_buf[group(g), :] = gather(g, own_table, 0, own_rows)
             return carry
 
-        lax.fori_loop(0, cell_groups, take_own, 0)
+        lax.fori_loop(0, cell_groups, take_own, 0, unroll=UNROLL)
         con_own = [gather(con_base + h, own_table, 0, own_rows) for h in range(con_rows)]
         for j in range(blocks):
             out_copy(turn, j).wait()
@@ -335,7 +336,7 @@
             cell_buf[group(g), :] += gather(g, ghost_table, own_rows, far_rows)
             return carry
 
-        lax.fori_loop(0, cell_groups, take_far, 0)
+        lax.fori_loop(0, cell_groups, take_far, 0, unroll=UNROLL)
         nodal = cell_buf[...]
         contrib = scale * jnp.dot(
             stiff_ref[...],
@@ -354,7 +355,7 @@
             ghost_acc[...] += scatter(g, cell_buf[group(g), :], own_rows, far_rows)
             return carry
 
-        lax.fori_loop(0, cell_groups, give_far, 0)
+        lax.fori_loop(0, cell_groups, give_far, 0, unroll=UNROLL)
         summed = folded(ghost_acc[...])
         spread = summed[0:ghost_rows]
         shares = []
@@ -373,7 +374,7 @@
             own_acc[...] += scatter(g, cell_buf[group(g), :], 0, own_rows)
             return carry
 
-        lax.fori_loop(0, cell_groups, give_own, 0)
+        lax.fori_loop(0, cell_groups, give_own, 0, unroll=UNROLL)
         both = own_acc[...]
         for h in range(con_rows):
             both = both + scatter(con_base + h, shares[h], 0, own_rows)

time: 64.2 us -> 51.6 us (0.80)
  Pallas kernels: 61.4 us -> 48.7 us
    pallas_call x1, Pallas kernels: 61.4 us -> 48.7 us  [on_device(): pl.pallas_call(functools.partial(kernel, shape, interp), out_shape=(tile,...]
where the time goes in v3:
time: 51.6 us; the launch traced here: 51.4 us
  Pallas kernels  48.7 us (94%)
  local copies, waits for them, and re-layouts  2 us (4%)
  between operations  0.65 us (1%)
    pallas_call x1, Pallas kernels, on_device(): pl.pallas_call(functools.partial(kernel, shape, interp), out_shape=(tile,...  48.7 us
    unnamed x4, local copies, waits for them, and re-layouts  2 us

profile of v3, /device:TPU:0, one launch (start us, length us, event | category | flops | bytes accessed | tf_op | source)
XLA Modules:
  0.0 51.4 jit_solution(13296152997879005863)
XLA Ops:
  0.6 48.7 %shard_map.95 = (f32[64,128]{1,0:T(8,128)}, f32[64,128]{1,0:T(8,128)}) custom-call(f32[64,128]{1,0:T(8,128)} %bitcast.6, f32[64,128]{1,0:T(8,128)} %bitcast.7, s32[125,128]{1,0:T(8,128)} %refs_2_.1, s32[1,128]{1,0:T(1,128)} %bitcast.11, s32[5,256]{1,0:T(8,128)} %refs_4_.1, s32[2,128]{1,0:T(2,128)} %bitcast.10, s32[8,512]{1,0:T(8,128)} %refs_6_.1, ...), custom_call_target="tpu_custom_call" | custom-call | tf_op jit(solution)/shard_map/pallas_call | solution.py:484
  49.3 0.0 copy-start
  49.4 1.4 %copy.12 = f32[8192]{0:T(1024)} copy(f32[8192]{0:T(1024)} %bitcast.9) | data formatting | bytes 65536
  50.7 0.0 copy-done
  50.7 0.6 %copy.13 = f32[8192]{0:T(1024)} copy(f32[8192]{0:T(1024)S(1)} %bitcast.8) | data formatting | bytes 65536
Async XLA Ops:
  49.3 1.4 %copy-start = (f32[64,128]{1,0:T(8,128)S(1)}, f32[64,128]{1,0:T(8,128)}, u32[]{:S(2)}) copy-start(f32[64,128]{1,0:T(8,128)} %get-tuple-element.5) | copy-start | bytes 98308
